TPU v7x, 64 devices: a 2x2x8 block of a 4x4x8 slice. The times are simulated.
64 devices in a mesh: dp: 4 (over x, y), tp: 16 (over z, core).
Axes of the slice: x: 2, y: 2, z: 8, core: 2. Of those that a mesh axis runs over, the one named last changes fastest.
The devices are a block of a 4x4x8 slice.
Arguments:
- x: bfloat16 [192, 64, 2560], P('dp'), parts along dimension 0
- g1: float32 [2, 2560], replicated
- g2: float32 [2, 2560], replicated
- wqkv: bfloat16 [2, 2560, 32, 240], P(None, None, 'tp')
- wo: bfloat16 [2, 2560, 2560], P(None, 'tp')
- w1: bfloat16 [2, 2560, 10240], P(None, None, 'tp')
- w2: bfloat16 [2, 10240, 2560], P(None, 'tp')
Outputs:
- output: bfloat16 [192, 64, 2560], P('dp'), parts along dimension 0
There are 4 independent parts. A program takes and returns all parts, laid end to end along the dimension named above; an argument that names none is the same for every part.
All inputs are finite; a program needn't handle non-finite values.
Results may differ from a plain program's by a relative error of at most 0.02.
Values are sent between devices in bfloat16 or wider.
A program may use at most 768 MiB of HBM per device.

v0:
```python
import jax
import jax.numpy as jnp
from jax import lax
from jax.sharding import PartitionSpec as P

EPS = 1e-5


def _ln(x, g):
    xf = x.astype(jnp.float32)
    mu = jnp.mean(xf, axis=-1, keepdims=True)
    var = jnp.mean(jnp.square(xf - mu), axis=-1, keepdims=True)
    return ((xf - mu) * lax.rsqrt(var + EPS) * g).astype(jnp.bfloat16)


def _attention(qkv):
    s = qkv.shape[1]
    hd = qkv.shape[-1]
    sc = jnp.einsum("bqhd,bkhd->bhqk", qkv[:, :, :, 0], qkv[:, :, :, 1], preferred_element_type=jnp.float32) * (hd ** -0.5)
    row = lax.broadcasted_iota(jnp.int32, (s, s), 0)
    col = lax.broadcasted_iota(jnp.int32, (s, s), 1)
    sc = jnp.where(row >= col, sc, -jnp.inf)
    p = jax.nn.softmax(sc, axis=-1).astype(jnp.bfloat16)
    return jnp.einsum("bhqk,bkhd->bqhd", p, qkv[:, :, :, 2], preferred_element_type=jnp.float32).astype(jnp.bfloat16)


def solution(mesh):
    def body(x, g1, g2, wqkv, wo, w1, w2):
        b, s, d = x.shape
        hl = wqkv.shape[2]
        hd = wqkv.shape[3] // 3
        h = x.reshape(b * s, d)
        for l in range(wqkv.shape[0]):
            a = _ln(h, g1[l])
            qkv = jnp.dot(a, wqkv[l].reshape(d, hl * 3 * hd), preferred_element_type=jnp.float32)
            qkv = qkv.astype(jnp.bfloat16).reshape(b, s, hl, 3, hd)
            o = _attention(qkv).reshape(b * s, hl * hd)
            pa = jnp.dot(o, wo[l], preferred_element_type=jnp.float32).astype(jnp.bfloat16)
            h = (h.astype(jnp.float32) + lax.psum(pa, "tp").astype(jnp.float32)).astype(jnp.bfloat16)
            m = jax.nn.gelu(jnp.dot(_ln(h, g2[l]), w1[l], preferred_element_type=jnp.float32), approximate=True).astype(jnp.bfloat16)
            pm = jnp.dot(m, w2[l], preferred_element_type=jnp.float32).astype(jnp.bfloat16)
            h = (h.astype(jnp.float32) + lax.psum(pm, "tp").astype(jnp.float32)).astype(jnp.bfloat16)
        return h.reshape(b, s, d)

    in_specs = (P("dp"), P(), P(), P(None, None, "tp", None), P(None, "tp", None), P(None, None, "tp"), P(None, "tp", None))
    return jax.shard_map(body, mesh=mesh, in_specs=in_specs, out_specs=P("dp"), check_vma=False)
```

profile of v0, /device:TPU:21, one launch (start us, length us, event | category | flops | bytes accessed | tf_op | source)
XLA Modules:
  0.0 1024.2 jit_solution(17609343359255334671)
XLA Ops:
  7.2 8.2 convert_reduce_fusion.3
  17.2 5.2 multiply_reduce_fusion
  22.6 2.5 fusion.122
  25.1 5.6 multiply_convert_fusion
  30.7 10.9 %convolution_convert_fusion.4 = bf16[3072,480]{0,1:T(8,128)(2,1)} fusion(bf16[3072,2560]{1,0:T(8,128)(2,1)S(1)} %bitcast.74, bf16[2560,480]{0,1:T(8,128)(2,1)} %bitcast.78), kind=kOutput, calls=%fused_computation.69 | convolution fusion | flops 7551221760 | bytes 21135360 | tf_op jit(solution)/shard_map/dot_general | solution.py:35
  41.6 8.2 reshape.97
  49.8 5.6 fusion.121
  55.4 4.2 copy.28
  59.7 3.3 copy.29
  63.0 2.7 copy.30
  65.8 2.5 fusion.83
  74.4 9.2 convolution_convert_fusion.3
  84.9 185.5 %all-reduce.5.cloned.1.call-done = bf16[3072,2560]{1,0:T(8,128)(2,1)} async-done(((bf16[3072,2560]{1,0:T(8,128)(2,1)}), bf16[3072,2560]{1,0:T(8,128)(2,1)}) %all-reduce.5.cloned.1.call-update) | async-done | bytes 15728656 | tf_op jit(solution)/shard_map/psum | solution.py:39
  270.4 13.3 %convert_reduce_fusion.2 = (f32[3072]{0:T(1024)S(1)}, bf16[3072,2560]{1,0:T(8,128)(2,1)S(1)}) fusion(bf16[3072,2560]{1,0:T(8,128)(2,1)} %all-reduce.5.cloned.1.call-done, bf16[48,64,2560]{2,1,0:T(8,128)(2,1)} %param.7), kind=kLoop, calls=%fused_computation.10 | loop fusion | flops 47182848 | bytes 47198208 | tf_op jit(solution)/shard_map/reduce_sum | solution.py:11
  283.8 5.9 fusion.14
  289.7 39.8 %convolution_convert_fusion.2 = bf16[3072,2560]{1,0:T(8,128)(2,1)} fusion(bf16[3072,2560]{1,0:T(8,128)(2,1)} %copy-done.2, f32[2560]{0:T(1024)S(1)} %get-tuple-element.6, f32[3072]{0:T(1024)S(1)} %add_rsqrt_fusion.3, f32[3072]{0:T(1024)S(1)} %broadcast_multiply_fusion.3, bf16[2,640,2560]{2,1,0:T(8,128)(2,1)} %param.13, bf16[2,2560,640]{2,1,0:T(8,128)(2,1)} %param.12), kind=kOutput, calls=%fused_computation.36 | convolution fusion | flops 20197539840 | bytes 38045696 | tf_op jit(solution)/shard_map/dot_general | solution.py:41
  329.7 181.3 %all-reduce.7.cloned.1.call-done = bf16[3072,2560]{1,0:T(8,128)(2,1)} async-done(((bf16[3072,2560]{1,0:T(8,128)(2,1)}), bf16[3072,2560]{1,0:T(8,128)(2,1)}) %all-reduce.7.cloned.1.call-update) | async-done | bytes 15728656 | tf_op jit(solution)/shard_map/psum | solution.py:42
  511.0 13.4 %convert_reduce_fusion.1 = (f32[3072]{0:T(1024)S(1)}, bf16[3072,2560]{1,0:T(8,128)(2,1)S(1)}) fusion(bf16[3072,2560]{1,0:T(8,128)(2,1)} %all-reduce.7.cloned.1.call-done, bf16[3072,2560]{1,0:T(8,128)(2,1)} %copy-done.2), kind=kLoop, calls=%fused_computation.7 | loop fusion | flops 47182848 | bytes 47198208 | tf_op jit(solution)/shard_map/reduce_sum | solution.py:11
  524.5 5.9 fusion.11
  530.6 9.2 fusion.56
  539.8 5.3 reshape.99
  545.1 5.6 fusion.120
  550.7 4.2 copy.31
  555.0 3.3 copy.32
  558.3 2.7 copy.33
  568.6 9.2 convolution_convert_fusion.1
  578.0 181.3 %all-reduce.9.cloned.1.call-done = bf16[3072,2560]{1,0:T(8,128)(2,1)} async-done(((bf16[3072,2560]{1,0:T(8,128)(2,1)}), bf16[3072,2560]{1,0:T(8,128)(2,1)}) %all-reduce.9.cloned.1.call-update) | async-done | bytes 15728656 | tf_op jit(solution)/shard_map/psum | solution.py:39
  759.3 13.3 %convert_reduce_fusion = (f32[3072]{0:T(1024)S(1)}, bf16[3072,2560]{1,0:T(8,128)(2,1)S(1)}) fusion(bf16[3072,2560]{1,0:T(8,128)(2,1)} %all-reduce.9.cloned.1.call-done, bf16[3072,2560]{1,0:T(8,128)(2,1)} %copy-done.1), kind=kLoop, calls=%fused_computation.4 | loop fusion | flops 47182848 | bytes 47198208 | tf_op jit(solution)/shard_map/reduce_sum | solution.py:11
  772.6 5.9 fusion.8
  778.6 39.8 %convolution_convert_fusion = bf16[3072,2560]{1,0:T(8,128)(2,1)} fusion(bf16[3072,2560]{1,0:T(8,128)(2,1)} %copy-done.3, f32[2560]{0:T(1024)S(1)} %copy-done.9, f32[3072]{0:T(1024)S(1)} %add_rsqrt_fusion.1, f32[3072]{0:T(1024)S(1)} %broadcast_multiply_fusion.1, bf16[2,640,2560]{2,1,0:T(8,128)(2,1)} %param.13, bf16[2,2560,640]{2,1,0:T(8,128)(2,1)} %param.12), kind=kOutput, calls=%fused_computation.34 | convolution fusion | flops 20197539840 | bytes 38045696 | tf_op jit(solution)/shard_map/dot_general | solution.py:41
  818.5 181.4 %all-reduce.11.cloned.1.call-done = bf16[3072,2560]{1,0:T(8,128)(2,1)} async-done(((bf16[3072,2560]{1,0:T(8,128)(2,1)}), bf16[3072,2560]{1,0:T(8,128)(2,1)}) %all-reduce.11.cloned.1.call-update) | async-done | bytes 15728656 | tf_op jit(solution)/shard_map/psum | solution.py:42
  999.9 17.3 %fusion.19 = bf16[3072,2560]{1,0:T(8,128)(2,1)} fusion(bf16[3072,2560]{1,0:T(8,128)(2,1)} %copy-done.3, bf16[3072,2560]{1,0:T(8,128)(2,1)} %all-reduce.11.cloned.1.call-done), kind=kLoop, calls=%fused_computation.28 | loop fusion | flops 31457280 | bytes 47185920 | tf_op jit(solution)/shard_map/convert_element_type | solution.py:42
  (55 shorter events, 18.0 us)
Async XLA Ops:
  6.5 263.9 %all-reduce.5.cloned.1.call-start = ((), (), s32[]{:S(2)}) async-start(), calls=%async_computation | async-start | bytes 31457280 | tf_op jit(solution)/shard_map/psum | solution.py:39
  7.2 10.1 copy-start
  7.2 15.4 %slice-start = ((s8[4915200]{0:T(1024)(128)(4,1)}), s8[4194304]{0:T(1024)(128)(4,1)S(1)}, s32[]{:S(2)}) async-start(s8[4915200]{0:T(1024)(128)(4,1)} %bitcast.75), calls=%async_computation.4 | async-start | bytes 8388608
  17.2 5.2 copy-start.7
  17.2 5.3 slice-start.1
  65.8 4.4 copy-start.6
  83.6 0.7 copy-start.8
  83.6 427.4 %all-reduce.7.cloned.1.call-start = ((), (), s32[]{:S(2)}) async-start(), calls=%async_computation.1 | async-start | bytes 31457280 | tf_op jit(solution)/shard_map/psum | solution.py:42
  283.7 5.9 copy-start.2
  329.6 429.7 %all-reduce.9.cloned.1.call-start = ((), (), s32[]{:S(2)}) async-start(), calls=%async_computation.2 | async-start | bytes 31457280 | tf_op jit(solution)/shard_map/psum | solution.py:39
  524.5 6.1 copy-start.1
  524.5 6.1 copy-start.4
  550.7 12.8 %copy-start.10 = (pred[64,64]{0,1:T(8,128)(4,1)S(1)}, pred[64,64]{0,1:T(8,128)(4,1)}, u32[]{:S(2)}) copy-start(pred[64,64]{0,1:T(8,128)(4,1)} %iota_compare_fusion) | copy-start | bytes 12292
  561.1 3.5 copy-start.5
  577.9 422.0 %all-reduce.11.cloned.1.call-start = ((), (), s32[]{:S(2)}) async-start(), calls=%async_computation.3 | async-start | bytes 31457280 | tf_op jit(solution)/shard_map/psum | solution.py:42
  772.6 6.0 copy-start.3
  772.6 6.0 copy-start.9
Sparse Core Ops, SparseCore 0:
  83.8 186.6 all-reduce.4
  329.7 181.2 all-reduce.6
  578.0 181.2 all-reduce.8
  818.6 181.2 all-reduce.10
where the time goes:
time: 1030 us; the launch traced here: 1020 us
  waiting for transfers between devices  730 us (71%)
  matrix products  125 us (12%)
  other arithmetic  97.7 us (9%)
  local copies, waits for them, and re-layouts  58.1 us (6%)
  between operations  13.8 us (1%)
    psum x2, waiting for transfers between devices, body(): lax.psum(pa, 'tp').astype(jnp.float32)  367 us
    psum x2, waiting for transfers between devices, body(): lax.psum(pm, 'tp').astype(jnp.float32)  363 us
    dot_general x2, matrix products, body(): jnp.dot(m, w2[l], preferred_element_type=jnp.float32).astype(jnp.bfloat16)  79.7 us
    reduce_sum x4, other arithmetic, _ln(): mu = jnp.mean(xf, axis=-1, keepdims=True)  48.2 us
    unnamed x32, local copies, waits for them, and re-layouts  23.3 us
    reduce_sum x4, other arithmetic, _ln(): var = jnp.mean(jnp.square(xf - mu), axis=-1, keepdims=True)  23 us
  transfers between devices with their start and end apart: 4, of which 4 were waited for; matrix products, arithmetic and copies ran while one was open for 0% of the time, Pallas kernels for 0%

commit v1 on v0

v1 whole, which is shorter than its diff:
```python
import functools

import jax
import jax.numpy as jnp
from jax import lax
from jax.experimental import pallas as pl
from jax.experimental.pallas import tpu as pltpu
from jax.sharding import PartitionSpec as P

EPS = 1e-5
MESH = pl.DeviceIdType.MESH
F32 = jnp.float32
BF16 = jnp.bfloat16
VMEM_LIMIT = 62 * 1024 * 1024


def _dot(a, b, ca, cb):
    return lax.dot_general(a, b, (((ca,), (cb,)), ((), ())), preferred_element_type=F32)


def _ln_rows(load, store, g, rows):
    def body(i, _):
        r = pl.ds(pl.multiple_of(i * 16, 16), 16)
        xf = load(r).astype(F32)
        d = xf - jnp.mean(xf, axis=-1, keepdims=True)
        var = jnp.mean(d * d, axis=-1, keepdims=True)
        store(r, (d * lax.rsqrt(var + EPS) * g).astype(BF16))
        return 0

    lax.fori_loop(0, rows // 16, body, 0)


def _place(nz):
    t = lax.axis_index("tp")
    z, c = t // 2, t % 2
    return t, z, c


def _chip(z, c, nz, sign, steps):
    fwd = sign * (1 - 2 * c) * steps
    return ((z + fwd + 8 * nz) % nz) * 2 + c


def _barrier(ids):
    sem = pltpu.get_barrier_semaphore()
    for i in ids:
        pl.semaphore_signal(sem, inc=1, device_id={"tp": i}, device_id_type=MESH)
    pl.semaphore_wait(sem, len(ids))


def _ring_kernel(kind, layer, nz, streams, *refs):
    (x_ref, g_ref, wa_ref, wb_ref, out_ref,
     abuf, pbuf, rbuf, wa, wb, own32, p32, mid, mid2,
     x_sem, w_sem, wsend_sem, wrecv_sem, ag_send, ag_recv, rs_send, rs_recv) = refs
    gather = kind != "att0"
    attention = kind != "mlp"
    t, z, c = _place(nz)
    nxt = [_chip(z, c, nz, sg, 1) for _, _, sg in streams]
    peer = t + 1 - 2 * c
    rows, width = own32.shape
    last = nz - 1

    _barrier([_chip(z, c, nz, 1, 1), _chip(z, c, nz, -1, 1), peer])

    own_w, send_w = [], []
    for i, (src, dst) in enumerate(((wa_ref, wa), (wb_ref, wb))):
        src = src.at[layer]
        if kind == "mlp" and i == 0:
            n = src.shape[1]
            lo, hi = dst.at[:, pl.ds(0, n)], dst.at[:, pl.ds(n, n)]
        else:
            n = src.shape[0]
            lo, hi = dst.at[pl.ds(0, n)], dst.at[pl.ds(n, n)]
        own_w.append(pltpu.make_async_copy(src, lo, w_sem.at[i]))
        send_w.append(pltpu.make_async_remote_copy(
            src_ref=src, dst_ref=hi, send_sem=wsend_sem.at[i], recv_sem=wrecv_sem.at[i],
            device_id={"tp": peer}, device_id_type=MESH))

    def x_copy(k, s):
        r0, nr, sg = streams[k]
        dev = _chip(z, c, nz, -sg, s)
        src = x_ref.at[pl.ds(pl.multiple_of(dev * rows + r0, 32), nr)]
        return pltpu.make_async_copy(src, abuf.at[s, pl.ds(r0, nr)], x_sem.at[k, s])

    def ag_copy(k, s):
        r0, nr, _ = streams[k]
        r = pl.ds(r0, nr)
        return pltpu.make_async_remote_copy(
            src_ref=abuf.at[s, r], dst_ref=abuf.at[s + 1, r], send_sem=ag_send.at[k, s], recv_sem=ag_recv.at[k, s + 1],
            device_id={"tp": nxt[k]}, device_id_type=MESH)

    def rs_copy(k, s):
        r0, nr, _ = streams[k]
        r = pl.ds(r0, nr)
        return pltpu.make_async_remote_copy(
            src_ref=pbuf.at[s, r], dst_ref=rbuf.at[s, r], send_sem=rs_send.at[k, s], recv_sem=rs_recv.at[k, s],
            device_id={"tp": nxt[k]}, device_id_type=MESH)

    ks = range(len(streams))
    g = g_ref[pl.ds(layer, 1), :]
    if not gather:
        for i in range(nz):
            for k in ks:
                x_copy(k, (i + 1) % nz).start()
    for w in own_w + send_w:
        w.start()
    if gather:
        _ln_rows(lambda r: x_ref[r, :], lambda r, v: abuf.__setitem__((0, r), v), g, rows)
        for k in ks:
            ag_copy(k, 0).start()
        own32[...] = x_ref[...].astype(F32)
    for w in own_w:
        w.wait()
    for w in send_w:
        w.wait_recv()

    if attention:
        hd = wb.shape[0] // (2 * 2)
        key = lax.broadcasted_iota(jnp.int32, (rows, rows), 0)
        query = lax.broadcasted_iota(jnp.int32, (rows, rows), 1)
        seq = rows // 3
        visible = (key <= query) & (key // seq == query // seq)

    def partial_sum(s):
        if attention:
            mid[...] = _dot(wa[...], abuf[s], 1, 1).astype(BF16)

            def head(h, _):
                base = h * (3 * hd)
                q = mid[pl.ds(pl.multiple_of(base, 16), hd), :]
                k = mid[pl.ds(pl.multiple_of(base + hd, 16), hd), :]
                v = mid[pl.ds(pl.multiple_of(base + 2 * hd, 16), hd), :]
                sc = _dot(k, q, 0, 0) * (hd ** -0.5)
                sc = jnp.where(visible, sc, -jnp.inf)
                e = jnp.exp(sc - jnp.max(sc, axis=0, keepdims=True))
                p = (e / jnp.sum(e, axis=0, keepdims=True)).astype(BF16)
                mid2[pl.ds(pl.multiple_of(h * hd, 16), hd), :] = _dot(v, p, 1, 0).astype(BF16)
                return 0

            lax.fori_loop(0, 4, head, 0)
            tile = 512

            def cols(n, _):
                cc = pl.ds(pl.multiple_of(n * tile, tile), tile)
                p32[:, cc] = _dot(mid2[...], wb[:, cc], 0, 0)
                return 0

            lax.fori_loop(0, width // tile, cols, 0)
        else:
            t1, t2 = 256, 512

            def hidden(n, _):
                cc = pl.ds(pl.multiple_of(n * t1, t1), t1)
                mid[:, cc] = jax.nn.gelu(_dot(abuf[s], wa[:, cc], 1, 0), approximate=True).astype(BF16)
                return 0

            lax.fori_loop(0, mid.shape[1] // t1, hidden, 0)

            def cols(n, _):
                cc = pl.ds(pl.multiple_of(n * t2, t2), t2)
                p32[:, cc] = _dot(mid[...], wb[:, cc], 1, 0)
                return 0

            lax.fori_loop(0, width // t2, cols, 0)

    def step(i, _):
        s = i if gather else i + ((9 - i) // 8) * (1 - 2 * i)

        if gather:
            @pl.when(s > 0)
            def _():
                for k in ks:
                    ag_copy(k, s - 1).wait_recv()

                    @pl.when(s < last)
                    def _():
                        ag_copy(k, s).start()
        else:
            for k in ks:
                x_copy(k, s).wait()

            @pl.when(s == 0)
            def _():
                own32[...] = abuf[0].astype(F32)

            _ln_rows(lambda r: abuf[s, r], lambda r, v: abuf.__setitem__((s, r), v), g, rows)

        partial_sum(s)

        @pl.when(s == 0)
        def _():
            own32[...] += p32[...]

        @pl.when(s > 0)
        def _():
            for k in ks:
                r0, nr, _ = streams[k]
                r = pl.ds(r0, nr)

                @pl.when(s == 1)
                def _():
                    pbuf[s, r] = p32[r, :].astype(BF16)

                @pl.when(s > 1)
                def _():
                    rs_copy(k, s - 1).wait_recv()
                    pbuf[s, r] = (p32[r, :] + rbuf[s - 1, r].astype(F32)).astype(BF16)

                rs_copy(k, s).start()

        return 0

    lax.fori_loop(0, nz, step, 0)

    for k in ks:
        r0, nr, _ = streams[k]
        r = pl.ds(r0, nr)
        rs_copy(k, last).wait_recv()
        out_ref[r, :] = (own32[r, :] + rbuf[last, r].astype(F32)).astype(BF16)

    def drain(s, _):
        for k in ks:
            rs_copy(k, s).wait_send()
            if gather:
                ag_copy(k, s - 1).wait_send()
        return 0

    lax.fori_loop(1, nz, drain, 0)
    for w in send_w:
        w.wait_send()


def _ring_call(kind, layer, nz, cid, x, g, wa, wb, rows, width):
    fine = ((0, rows // 3, 1), (rows // 3, rows // 3, 1), (2 * rows // 3, rows // 6, -1), (5 * rows // 6, rows // 6, -1))
    coarse = ((0, 2 * rows // 3, 1), (2 * rows // 3, rows // 3, -1))
    streams = fine if kind == "att0" else coarse
    nk = len(streams)
    big = pltpu.VMEM((nz, rows, width), BF16)
    if kind == "mlp":
        wshape = ((width, 2 * wa.shape[2]), (2 * wb.shape[1], width))
        mids = ((rows, 2 * wa.shape[2]), (16, 128))
    else:
        wshape = ((2 * wa.shape[1], width), (2 * wb.shape[1], width))
        mids = ((2 * wa.shape[1], rows), (2 * wb.shape[1], rows))
    vmem, hbm = pl.BlockSpec(memory_space=pltpu.VMEM), pl.BlockSpec(memory_space=pl.ANY)
    dma = pltpu.SemaphoreType.DMA
    return pl.pallas_call(
        functools.partial(_ring_kernel, kind, layer, nz, streams),
        out_shape=jax.ShapeDtypeStruct((rows, width), BF16),
        in_specs=[hbm if kind == "att0" else vmem, vmem, hbm, hbm],
        out_specs=vmem,
        scratch_shapes=[
            big, big, big, pltpu.VMEM(wshape[0], BF16), pltpu.VMEM(wshape[1], BF16),
            pltpu.VMEM((rows, width), F32), pltpu.VMEM((rows, width), F32),
            pltpu.VMEM(mids[0], BF16), pltpu.VMEM(mids[1], BF16),
            dma((nk, nz)), dma((2,)), dma((2,)), dma((2,)),
            dma((nk, nz)), dma((nk, nz)), dma((nk, nz)), dma((nk, nz)),
        ],
        compiler_params=pltpu.CompilerParams(collective_id=cid, has_side_effects=True, vmem_limit_bytes=VMEM_LIMIT),
        name=f"{kind}_{layer}",
    )(x, g, wa, wb)


def _gather_kernel(nz, streams, x_ref, out_ref, buf, loc_sem, send_sem, recv_sem, psend_sem, precv_sem):
    t, z, c = _place(nz)
    nxt = [_chip(z, c, nz, sg, 1) for _, _, sg in streams]
    peer = t + 1 - 2 * c
    rows = x_ref.shape[0]
    ks = range(len(streams))
    last = nz - 1
    _barrier([_chip(z, c, nz, 1, 1), _chip(z, c, nz, -1, 1), peer])

    def src(k, s):
        r0, nr, _ = streams[k]
        return buf.at[s, pl.ds(r0, nr)]

    def spot(k, s, core):
        r0, nr, sg = streams[k]
        dev = _chip(z, core, nz, -sg * (1 - 2 * c) * (1 - 2 * core), s)
        return out_ref.at[pl.ds(pl.multiple_of(dev * rows + r0, 32), nr)]

    def ring(k, s):
        return pltpu.make_async_remote_copy(
            src_ref=src(k, s), dst_ref=src(k, s + 1), send_sem=send_sem.at[k, s], recv_sem=recv_sem.at[k, s + 1],
            device_id={"tp": nxt[k]}, device_id_type=MESH)

    def local(k, s):
        return pltpu.make_async_copy(src(k, s), spot(k, s, c), loc_sem.at[k, s])

    def across(k, s):
        return pltpu.make_async_remote_copy(
            src_ref=src(k, s), dst_ref=spot(k, s, c), send_sem=psend_sem.at[k, s], recv_sem=precv_sem.at[k, s],
            device_id={"tp": peer}, device_id_type=MESH)

    own = pltpu.make_async_copy(x_ref, buf.at[0], loc_sem.at[0, 0])
    own.start()
    own.wait()
    for k in ks:
        ring(k, 0).start()
    for k in ks:
        local(k, 0).start()
        across(k, 0).start()

    def step(s, _):
        for k in ks:
            ring(k, s - 1).wait_recv()

            @pl.when(s < last)
            def _():
                ring(k, s).start()

            local(k, s).start()
            across(k, s).start()
        return 0

    lax.fori_loop(1, nz, step, 0)

    def drain(s, _):
        for k in ks:
            local(k, s).wait()
            across(k, s).wait()

            @pl.when(s < last)
            def _():
                ring(k, s).wait_send()
        return 0

    lax.fori_loop(0, nz, drain, 0)


def _gather_call(nz, cid, x):
    rows, width = x.shape
    streams = ((0, rows // 3, 1), (rows // 3, rows // 3, 1), (2 * rows // 3, rows // 6, -1), (5 * rows // 6, rows // 6, -1))
    nk = len(streams)
    dma = pltpu.SemaphoreType.DMA
    hbm = pl.BlockSpec(memory_space=pl.ANY)
    return pl.pallas_call(
        functools.partial(_gather_kernel, nz, streams),
        out_shape=jax.ShapeDtypeStruct((2 * nz * rows, width), BF16),
        in_specs=[hbm],
        out_specs=hbm,
        scratch_shapes=[pltpu.VMEM((nz, rows, width), BF16)] + [dma((nk, nz))] * 5,
        compiler_params=pltpu.CompilerParams(collective_id=cid, has_side_effects=True, vmem_limit_bytes=VMEM_LIMIT),
        name="gather",
    )(x)


def solution(mesh):
    n = mesh.shape["tp"]
    nz = n // 2

    def body(x, g1, g2, wqkv, wo, w1, w2):
        b, s, d = x.shape
        rows = b * s // n
        layers, _, hl, hd3 = wqkv.shape
        wt = wqkv.transpose(0, 2, 3, 1).reshape(layers, hl * hd3, d)
        h = x.reshape(b * s, d)
        cid = 0
        for l in range(layers):
            h = _ring_call("att0" if l == 0 else "att", l, nz, cid, h, g1, wt, wo, rows, d)
            h = _ring_call("mlp", l, nz, cid + 1, h, g2, w1, w2, rows, d)
            cid += 2
        return _gather_call(nz, cid, h).reshape(b, s, d)

    in_specs = (P("dp"), P(), P(), P(None, None, "tp", None), P(None, "tp", None), P(None, None, "tp"), P(None, "tp", None))
    return jax.shard_map(body, mesh=mesh, in_specs=in_specs, out_specs=P("dp"), check_vma=False)
```

time: 1030 us -> 683 us (0.66)
  waiting for transfers between devices: 730 us -> 0 us
  Pallas kernels: 0 us -> 669 us
  matrix products: 125 us -> 0 us
  other arithmetic: 97.7 us -> 0 us
  local copies, waits for them, and re-layouts: 58.1 us -> 13.3 us
  between operations: 13.8 us -> 0.04 us
    psum x4 -> x0, waiting for transfers between devices: 730 us -> none  [the longest x2 367 us: body(): lax.psum(pa, 'tp').astype(jnp.float32)]
    pallas_call x0 -> x5, Pallas kernels: none -> 669 us  [the longest x4 587 us: _ring_call(): pl.pallas_call(functools.partial(_ring_kernel, kind, layer, nz, streams),...]
    dot_general x10 -> x0, matrix products: 125 us -> none  [the longest x2 79.7 us: body(): jnp.dot(m, w2[l], preferred_element_type=jnp.float32).astype(jnp.bfloat16)]
    reduce_sum x8 -> x0, other arithmetic: 71.2 us -> none  [the longest x4 48.2 us: _ln(): mu = jnp.mean(xf, axis=-1, keepdims=True)]
    convert_element_type x2 -> x0, other arithmetic: 22.9 us -> none  [the longest x1 17.3 us: body(): (h.astype(jnp.float32) + lax.psum(pm, 'tp').astype(jnp.float32)).astype(j...]
    reshape x4 -> x0, local copies, waits for them, and re-layouts: 16.8 us -> none  [the longest x2 13.5 us: body(): qkv = qkv.astype(jnp.bfloat16).reshape(b, s, hl, 3, hd)]
    slice x5 -> x0, local copies, waits for them, and re-layouts: 14.5 us -> none  [the longest x2 11.3 us: _attention(): qkv[:, :, :, 2]]
    unnamed x32 -> x1, local copies, waits for them, and re-layouts: 23.3 us -> 13.3 us
  transfers between devices with their start and end apart: 4 -> 0, of which waited for: 4 -> 0; matrix products, arithmetic and copies ran while one was open for 0% -> 0% of each run, Pallas kernels for 0% -> 0%
where the time goes in v1:
time: 683 us
  Pallas kernels  669 us (98%)
  local copies, waits for them, and re-layouts  13.3 us (2%)
    pallas_call x4, Pallas kernels, _ring_call(): pl.pallas_call(functools.partial(_ring_kernel, kind, layer, nz, streams),...  587 us
    pallas_call x1, Pallas kernels, _gather_call(): pl.pallas_call(functools.partial(_gather_kernel, nz, streams), out_shape=...  82.3 us

profile of v1, /device:TPU:21, one launch (start us, length us, event | category | flops | bytes accessed | tf_op | source)
XLA Modules:
  0.0 682.7 jit_solution(2051096199474434124)
XLA Ops:
  0.0 104.7 %att0_0.1.refs_0_ = bf16[192,2560]{1,0:T(8,128)(2,1)} custom-call(bf16[3072,2560]{1,0:T(8,128)(2,1)} %bitcast.8, f32[2,2560]{1,0:T(2,128)} %refs_1_.6, bf16[2,480,2560]{2,1,0:T(8,128)(2,1)} %bitcast.6, bf16[2,160,2560]{2,1,0:T(8,128)(2,1)} %refs_3_.6), custom_call_target="tpu_custom_call" | custom-call | tf_op jit(solution)/shard_map/att0_0/pallas_call | solution.py:247
  104.7 160.9 %mlp_0.1.refs_0_ = bf16[192,2560]{1,0:T(8,128)(2,1)} custom-call(bf16[192,2560]{1,0:T(8,128)(2,1)} %att0_0.1.refs_0_, f32[2,2560]{1,0:T(2,128)} %refs_1_.7, bf16[2,2560,640]{2,1,0:T(8,128)(2,1)} %refs_2_.3, bf16[2,640,2560]{2,1,0:T(8,128)(2,1)} %refs_3_.7), custom_call_target="tpu_custom_call" | custom-call | tf_op jit(solution)/shard_map/mlp_0/pallas_call | solution.py:247
  265.6 160.6 %att_1.1.refs_0_ = bf16[192,2560]{1,0:T(8,128)(2,1)} custom-call(bf16[192,2560]{1,0:T(8,128)(2,1)} %mlp_0.1.refs_0_, f32[2,2560]{1,0:T(2,128)} %refs_1_.6, bf16[2,480,2560]{2,1,0:T(8,128)(2,1)} %bitcast.7, bf16[2,160,2560]{2,1,0:T(8,128)(2,1)} %refs_3_.6), custom_call_target="tpu_custom_call" | custom-call | tf_op jit(solution)/shard_map/att_1/pallas_call | solution.py:247
  426.2 160.9 %mlp_1.1.x_ref = bf16[192,2560]{1,0:T(8,128)(2,1)} custom-call(bf16[192,2560]{1,0:T(8,128)(2,1)} %att_1.1.refs_0_, f32[2,2560]{1,0:T(2,128)} %refs_1_.7, bf16[2,2560,640]{2,1,0:T(8,128)(2,1)} %refs_2_.3, bf16[2,640,2560]{2,1,0:T(8,128)(2,1)} %refs_3_.7), custom_call_target="tpu_custom_call" | custom-call | tf_op jit(solution)/shard_map/mlp_1/pallas_call | solution.py:247
  587.1 82.3 %gather.1 = bf16[3072,2560]{1,0:T(8,128)(2,1)} custom-call(bf16[192,2560]{1,0:T(8,128)(2,1)} %mlp_1.1.x_ref), custom_call_target="tpu_custom_call" | custom-call | tf_op jit(solution)/shard_map/gather/pallas_call | solution.py:337
  669.4 13.3 %copy.9 = bf16[48,64,2560]{2,1,0:T(8,128)(2,1)} copy(bf16[48,64,2560]{2,1,0:T(8,128)(2,1)} %bitcast.5) | data formatting | bytes 31457280

commit v2 on v1

--- a/solution.py
+++ b/solution.py
@@ -1,4 +1,5 @@
 import functools
+import math
 
 import jax
 import jax.numpy as jnp
@@ -41,17 +42,103 @@
     return ((z + fwd + 8 * nz) % nz) * 2 + c
 
 
-def _barrier(ids):
+def _barrier(ids, nd=1):
     sem = pltpu.get_barrier_semaphore()
     for i in ids:
         pl.semaphore_signal(sem, inc=1, device_id={"tp": i}, device_id_type=MESH)
-    pl.semaphore_wait(sem, len(ids))
-
-
-def _ring_kernel(kind, layer, nz, streams, *refs):
+    if nd > 1:
+        d = lax.axis_index("dp")
+
+        def one(e, _):
+            pl.semaphore_signal(sem, inc=1, device_id={"dp": (d + e) % nd, "tp": lax.axis_index("tp")}, device_id_type=MESH)
+            return 0
+
+        lax.fori_loop(1, nd, one, 0)
+    pl.semaphore_wait(sem, len(ids) + nd - 1)
+
+
+def _block(ref, d, nd, rows, cols):
+    a = math.gcd(nd, 20)
+    b = nd // a
+    r, c = rows // a, cols // b
+    return ref.at[pl.ds(pl.multiple_of((d // b) * r, 8), r), pl.ds(pl.multiple_of((d % b) * c, 128), c)]
+
+
+class _Prefetch:
+    def __init__(self, nz, nd, place, srcs, dsts, sems):
+        self.nz, self.nd = nz, nd
+        self.t, self.z, self.c = place
+        self.d = lax.axis_index("dp")
+        self.srcs, self.dsts = srcs, dsts
+        self.ring_send, self.ring_recv, self.peer_send, self.peer_recv = sems
+
+    def part(self, j, s, d):
+        sign = 1 - 2 * j
+        chip = _chip(self.z, self.c, self.nz, -sign, s) // 2
+        ref = self.dsts[j].at[chip]
+        return _block(ref, d, self.nd, ref.shape[0], ref.shape[1])
+
+    def ring(self, j, s, first=False):
+        if first:
+            ref = self.srcs[j]
+            src = _block(ref, self.d, self.nd, ref.shape[0], ref.shape[1])
+        else:
+            src = self.part(j, s, self.d)
+        return pltpu.make_async_remote_copy(
+            src_ref=src, dst_ref=self.part(j, s, self.d), send_sem=self.ring_send.at[j, s], recv_sem=self.ring_recv.at[j, s + 1],
+            device_id={"tp": _chip(self.z, self.c, self.nz, 1 - 2 * j, 1)}, device_id_type=MESH)
+
+    def peer(self, j, s, e):
+        mine = self.part(j, s, self.d)
+        return pltpu.make_async_remote_copy(
+            src_ref=mine, dst_ref=mine, send_sem=self.peer_send.at[j, s, e], recv_sem=self.peer_recv.at[j, s, e],
+            device_id={"dp": (self.d + e) % self.nd, "tp": self.t}, device_id_type=MESH)
+
+    def start_ring(self):
+        for j in (0, 1):
+            self.ring(j, 0, True).start()
+
+    def arrived(self, s):
+        for j in (0, 1):
+            self.ring(j, s - 1).wait_recv()
+
+            @pl.when(s < self.nz - 1)
+            def _():
+                self.ring(j, s).start()
+
+    def to_peers(self, s):
+        def one(e, _):
+            for j in (0, 1):
+                self.peer(j, s, e).start()
+            return 0
+
+        lax.fori_loop(1, self.nd, one, 0)
+
+    def drain_peers(self, lo, hi):
+        def one(i, _):
+            s, e = lo + i // (self.nd - 1), 1 + i % (self.nd - 1)
+            for j in (0, 1):
+                self.peer(j, s, e).wait()
+            return 0
+
+        lax.fori_loop(0, (hi - lo) * (self.nd - 1), one, 0)
+
+    def drain_ring(self):
+        def one(s, _):
+            for j in (0, 1):
+                self.ring(j, s).wait_send()
+            return 0
+
+        lax.fori_loop(0, self.nz - 1, one, 0)
+
+
+def _ring_kernel(kind, layer, nz, nd, streams, names, *refs):
+    r_ = dict(zip(names, refs, strict=True))
     (x_ref, g_ref, wa_ref, wb_ref, out_ref,
      abuf, pbuf, rbuf, wa, wb, own32, p32, mid, mid2,
-     x_sem, w_sem, wsend_sem, wrecv_sem, ag_send, ag_recv, rs_send, rs_recv) = refs
+     x_sem, w_sem, wsend_sem, wrecv_sem, ag_send, ag_recv, rs_send, rs_recv) = (r_[n] for n in (
+         "x", "g", "wa", "wb", "out", "abuf", "pbuf", "rbuf", "wa_v", "wb_v", "own32", "p32", "mid", "mid2",
+         "x_sem", "w_sem", "wsend", "wrecv", "ag_send", "ag_recv", "rs_send", "rs_recv"))
     gather = kind != "att0"
     attention = kind != "mlp"
     t, z, c = _place(nz)
@@ -60,7 +147,12 @@
     rows, width = own32.shape
     last = nz - 1
 
-    _barrier([_chip(z, c, nz, 1, 1), _chip(z, c, nz, -1, 1), peer])
+    pre = None
+    split = (nz + 1) // 2
+    if "gq" in r_:
+        pre = _Prefetch(nz, nd, (t, z, c), [r_[n].at[layer + 1] for n in ("pa", "pb") if n in r_], [r_["gq"], r_["go"]],
+                        [r_[n] for n in ("pr_send", "pr_recv", "pp_send", "pp_recv")])
+    _barrier([_chip(z, c, nz, 1, 1), _chip(z, c, nz, -1, 1), peer], nd if pre else 1)
 
     own_w, send_w = [], []
     for i, (src, dst) in enumerate(((wa_ref, wa), (wb_ref, wb))):
@@ -102,6 +194,8 @@
         for i in range(nz):
             for k in ks:
                 x_copy(k, (i + 1) % nz).start()
+    if pre and not gather:
+        pre.start_ring()
     for w in own_w + send_w:
         w.start()
     if gather:
@@ -163,6 +257,9 @@
 
             lax.fori_loop(0, width // t2, cols, 0)
 
+    if pre and gather:
+        lax.fori_loop(split, nz, lambda s, _: (pre.to_peers(s), 0)[1], 0)
+
     def step(i, _):
         s = i if gather else i + ((9 - i) // 8) * (1 - 2 * i)
 
@@ -176,6 +273,14 @@
                     def _():
                         ag_copy(k, s).start()
         else:
+            if pre:
+                @pl.when(i > 0)
+                def _():
+                    pre.arrived(i)
+
+                    @pl.when(i < split)
+                    def _():
+                        pre.to_peers(i)
             for k in ks:
                 x_copy(k, s).wait()
 
@@ -228,9 +333,15 @@
     lax.fori_loop(1, nz, drain, 0)
     for w in send_w:
         w.wait_send()
-
-
-def _ring_call(kind, layer, nz, cid, x, g, wa, wb, rows, width):
+    if pre:
+        if gather:
+            pre.drain_peers(split, nz)
+        else:
+            pre.drain_ring()
+            pre.drain_peers(1, split)
+
+
+def _ring_call(kind, layer, nz, nd, cid, x, g, wa, wb, rows, width, prefetch=False, gathered=None):
     fine = ((0, rows // 3, 1), (rows // 3, rows // 3, 1), (2 * rows // 3, rows // 6, -1), (5 * rows // 6, rows // 6, -1))
     coarse = ((0, 2 * rows // 3, 1), (2 * rows // 3, rows // 3, -1))
     streams = fine if kind == "att0" else coarse
@@ -244,21 +355,156 @@
         mids = ((2 * wa.shape[1], rows), (2 * wb.shape[1], rows))
     vmem, hbm = pl.BlockSpec(memory_space=pltpu.VMEM), pl.BlockSpec(memory_space=pl.ANY)
     dma = pltpu.SemaphoreType.DMA
+    ins = [("x", x, hbm if kind == "att0" else vmem), ("g", g, vmem), ("wa", wa, hbm), ("wb", wb, hbm)]
+    outs = [("out", jax.ShapeDtypeStruct((rows, width), BF16), vmem)]
+    alias = {}
+    if prefetch:
+        ins += [("pa", wa, hbm), ("pb", wb, hbm)]
+        outs += [("gq", jax.ShapeDtypeStruct((nz, *wa.shape[1:]), BF16), hbm), ("go", jax.ShapeDtypeStruct((nz, *wb.shape[1:]), BF16), hbm)]
+    if gathered:
+        for i, (n, a) in enumerate(zip(("gq", "go"), gathered)):
+            alias[len(ins)] = len(outs)
+            ins += [(n + "_in", a, hbm)]
+            outs += [(n, jax.ShapeDtypeStruct(a.shape, a.dtype), hbm)]
+    scratch = [
+        ("abuf", big), ("pbuf", big), ("rbuf", big), ("wa_v", pltpu.VMEM(wshape[0], BF16)), ("wb_v", pltpu.VMEM(wshape[1], BF16)),
+        ("own32", pltpu.VMEM((rows, width), F32)), ("p32", pltpu.VMEM((rows, width), F32)),
+        ("mid", pltpu.VMEM(mids[0], BF16)), ("mid2", pltpu.VMEM(mids[1], BF16)),
+        ("x_sem", dma((nk, nz))), ("w_sem", dma((2,))), ("wsend", dma((2,))), ("wrecv", dma((2,))),
+        ("ag_send", dma((nk, nz))), ("ag_recv", dma((nk, nz))), ("rs_send", dma((nk, nz))), ("rs_recv", dma((nk, nz))),
+    ]
+    if prefetch or gathered:
+        scratch += [("pr_send", dma((2, nz))), ("pr_recv", dma((2, nz))), ("pp_send", dma((2, nz, nd))), ("pp_recv", dma((2, nz, nd)))]
+    names = [e[0] for e in ins + outs + scratch]
+    res = pl.pallas_call(
+        functools.partial(_ring_kernel, kind, layer, nz, nd, streams, names),
+        out_shape=[e[1] for e in outs],
+        in_specs=[e[2] for e in ins],
+        out_specs=[e[2] for e in outs],
+        scratch_shapes=[e[1] for e in scratch],
+        input_output_aliases=alias,
+        compiler_params=pltpu.CompilerParams(collective_id=cid, has_side_effects=True, vmem_limit_bytes=VMEM_LIMIT),
+        name=f"{kind}_{layer}",
+    )(*[e[1] for e in ins])
+    return res if len(res) > 1 else res[0]
+
+
+def _local_kernel(layer, nz, x_ref, g_ref, wa_ref, wb_ref, gq_ref, go_ref, out_ref,
+                  abuf, pbuf, rbuf, wa, wb, own32, mid, ot, wa_sem, wb_sem, a_send, a_recv, p_send, p_recv):
+    t, z, c = _place(nz)
+    peer = t + 1 - 2 * c
+    rows, width = out_ref.shape
+    na, nb = wa_ref.shape[1], wb_ref.shape[1]
+    hd = na // 6
+    tiles = pbuf.shape[0]
+    _barrier([peer])
+
+    def load(j, chip, here=False):
+        dst, ref, own, sem = ((wa, gq_ref, wa_ref, wa_sem), (wb, go_ref, wb_ref, wb_sem))[j]
+        n = own.shape[1]
+        src = own.at[layer] if here else ref.at[chip]
+        return pltpu.make_async_copy(src, dst.at[pl.ds(pl.multiple_of(chip * n, 16), n)], sem.at[chip])
+
+    def start(j, chip):
+        @pl.when(chip == z)
+        def _():
+            load(j, chip, True).start()
+
+        @pl.when(chip != z)
+        def _():
+            load(j, chip).start()
+
+    for j in (0, 1):
+        lax.fori_loop(0, nz, lambda chip, _: (start(j, chip), 0)[1], 0)
+    g = g_ref[pl.ds(layer, 1), :]
+    _ln_rows(lambda r: x_ref[r, :], lambda r, v: abuf.__setitem__((r, slice(None)), v), g, rows)
+    swap = pltpu.make_async_remote_copy(
+        src_ref=abuf.at[pl.ds(0, rows)], dst_ref=abuf.at[pl.ds(rows, rows)], send_sem=a_send, recv_sem=a_recv,
+        device_id={"tp": peer}, device_id_type=MESH)
+    swap.start()
+    own32[...] = x_ref[...].astype(F32)
+    swap.wait_recv()
+
+    blk = 128
+    seq = rows // 3
+    key = lax.broadcasted_iota(jnp.int32, (blk, blk), 0)
+    query = lax.broadcasted_iota(jnp.int32, (blk, blk), 1)
+    visible = (key <= query) & (key // seq == query // seq)
+
+    def pair(i, _):
+        for k in (0, 1):
+            load(0, 2 * i + k).wait()
+        w = wa[pl.ds(pl.multiple_of(i * 2 * na, 16), 2 * na), :]
+        mid[...] = _dot(w, abuf[...], 1, 1).astype(BF16)
+
+        def head(h, _):
+            base = h * (3 * hd)
+            for b in range(2 * rows // blk):
+                cc = pl.ds(b * blk, blk)
+                q = mid[pl.ds(pl.multiple_of(base, 16), hd), cc]
+                k = mid[pl.ds(pl.multiple_of(base + hd, 16), hd), cc]
+                v = mid[pl.ds(pl.multiple_of(base + 2 * hd, 16), hd), cc]
+                sc = _dot(k, q, 0, 0) * (hd ** -0.5)
+                sc = jnp.where(visible, sc, -jnp.inf)
+                e = jnp.exp(sc - jnp.max(sc, axis=0, keepdims=True))
+                p = (e / jnp.sum(e, axis=0, keepdims=True)).astype(BF16)
+                ot[pl.ds(pl.multiple_of(i * 2 * nb + h * hd, 16), hd), cc] = _dot(v, p, 1, 0).astype(BF16)
+            return 0
+
+        lax.fori_loop(0, 4, head, 0)
+        return 0
+
+    lax.fori_loop(0, nz // 2, pair, 0)
+    lax.fori_loop(0, nz, lambda chip, _: (load(1, chip).wait(), 0)[1], 0)
+
+    def part(n):
+        return pltpu.make_async_remote_copy(
+            src_ref=pbuf.at[n], dst_ref=rbuf.at[n], send_sem=p_send.at[n], recv_sem=p_recv.at[n],
+            device_id={"tp": peer}, device_id_type=MESH)
+
+    tile = width // tiles
+
+    def cols(n, _):
+        cc = pl.ds(pl.multiple_of(n * tile, tile), tile)
+        p = _dot(ot[...], wb[:, cc], 0, 0)
+        pbuf[n] = p[rows:].astype(BF16)
+        part(n).start()
+        own32[:, cc] += p[:rows]
+        return 0
+
+    lax.fori_loop(0, tiles, cols, 0)
+
+    def last(n, _):
+        cc = pl.ds(pl.multiple_of(n * tile, tile), tile)
+        part(n).wait()
+        out_ref[:, cc] = (own32[:, cc] + rbuf[n].astype(F32)).astype(BF16)
+        return 0
+
+    lax.fori_loop(0, tiles, last, 0)
+    swap.wait_send()
+
+
+def _local_call(layer, nz, cid, x, g, wa, wb, gq, go):
+    rows, width = x.shape
+    na, nb = wa.shape[1], wb.shape[1]
+    tiles = 5
+    vmem, hbm = pl.BlockSpec(memory_space=pltpu.VMEM), pl.BlockSpec(memory_space=pl.ANY)
+    dma = pltpu.SemaphoreType.DMA
     return pl.pallas_call(
-        functools.partial(_ring_kernel, kind, layer, nz, streams),
+        functools.partial(_local_kernel, layer, nz),
         out_shape=jax.ShapeDtypeStruct((rows, width), BF16),
-        in_specs=[hbm if kind == "att0" else vmem, vmem, hbm, hbm],
+        in_specs=[vmem, vmem, hbm, hbm, hbm, hbm],
         out_specs=vmem,
         scratch_shapes=[
-            big, big, big, pltpu.VMEM(wshape[0], BF16), pltpu.VMEM(wshape[1], BF16),
-            pltpu.VMEM((rows, width), F32), pltpu.VMEM((rows, width), F32),
-            pltpu.VMEM(mids[0], BF16), pltpu.VMEM(mids[1], BF16),
-            dma((nk, nz)), dma((2,)), dma((2,)), dma((2,)),
-            dma((nk, nz)), dma((nk, nz)), dma((nk, nz)), dma((nk, nz)),
+            pltpu.VMEM((2 * rows, width), BF16), pltpu.VMEM((tiles, rows, width // tiles), BF16),
+            pltpu.VMEM((tiles, rows, width // tiles), BF16),
+            pltpu.VMEM((nz * na, width), BF16), pltpu.VMEM((nz * nb, width), BF16), pltpu.VMEM((rows, width), F32),
+            pltpu.VMEM((2 * na, 2 * rows), BF16), pltpu.VMEM((nz * nb, 2 * rows), BF16),
+            dma((nz,)), dma((nz,)), dma, dma, dma((tiles,)), dma((tiles,)),
         ],
         compiler_params=pltpu.CompilerParams(collective_id=cid, has_side_effects=True, vmem_limit_bytes=VMEM_LIMIT),
-        name=f"{kind}_{layer}",
-    )(x, g, wa, wb)
+        name=f"local_{layer}",
+    )(x, g, wa, wb, gq, go)
 
 
 def _gather_kernel(nz, streams, x_ref, out_ref, buf, loc_sem, send_sem, recv_sem, psend_sem, precv_sem):
@@ -348,6 +594,7 @@
 def solution(mesh):
     n = mesh.shape["tp"]
     nz = n // 2
+    nd = mesh.shape["dp"]
 
     def body(x, g1, g2, wqkv, wo, w1, w2):
         b, s, d = x.shape
@@ -355,11 +602,11 @@
         layers, _, hl, hd3 = wqkv.shape
         wt = wqkv.transpose(0, 2, 3, 1).reshape(layers, hl * hd3, d)
         h = x.reshape(b * s, d)
-        cid = 0
-        for l in range(layers):
-            h = _ring_call("att0" if l == 0 else "att", l, nz, cid, h, g1, wt, wo, rows, d)
-            h = _ring_call("mlp", l, nz, cid + 1, h, g2, w1, w2, rows, d)
-            cid += 2
+        h, gq, go = _ring_call("att0", 0, nz, nd, 0, h, g1, wt, wo, rows, d, prefetch=True)
+        h, gq, go = _ring_call("mlp", 0, nz, nd, 1, h, g2, w1, w2, rows, d, gathered=(gq, go))
+        h = _local_call(1, nz, 2, h, g1, wt, wo, gq, go)
+        h = _ring_call("mlp", 1, nz, nd, 3, h, g2, w1, w2, rows, d)
+        cid = 4
         return _gather_call(nz, cid, h).reshape(b, s, d)
 
     in_specs = (P("dp"), P(), P(), P(None, None, "tp", None), P(None, "tp", None), P(None, None, "tp"), P(None, "tp", None))

time: 683 us -> 610 us (0.89)
  Pallas kernels: 669 us -> 596 us
    pallas_call x4, Pallas kernels: 587 us -> 514 us  [the longest x3 481 us: _ring_call(): pl.pallas_call(functools.partial(_ring_kernel, kind, layer, nz, nd, strea...]
where the time goes in v2:
time: 610 us; the launch traced here: 609 us
  Pallas kernels  596 us (98%)
  local copies, waits for them, and re-layouts  13.3 us (2%)
    pallas_call x3, Pallas kernels, _ring_call(): pl.pallas_call(functools.partial(_ring_kernel, kind, layer, nz, nd, strea...  481 us
    pallas_call x1, Pallas kernels, _gather_call(): pl.pallas_call(functools.partial(_gather_kernel, nz, streams), out_shape=...  82.3 us
    pallas_call x1, Pallas kernels, _local_call(): pl.pallas_call(functools.partial(_local_kernel, layer, nz), out_shape=jax...  32.3 us
    unnamed x1, local copies, waits for them, and re-layouts  13.3 us

profile of v2, /device:TPU:21, one launch (start us, length us, event | category | flops | bytes accessed | tf_op | source)
XLA Modules:
  0.0 609.3 jit_solution(13147640116731953333)
XLA Ops:
  0.0 153.0 %att0_0.1 = (bf16[192,2560]{1,0:T(8,128)(2,1)}, bf16[8,480,2560]{2,1,0:T(8,128)(2,1)}, bf16[8,160,2560]{2,1,0:T(8,128)(2,1)}) custom-call(bf16[3072,2560]{1,0:T(8,128)(2,1)} %bitcast.9, f32[2,2560]{1,0:T(2,128)} %g_ref.1, bf16[2,480,2560]{2,1,0:T(8,128)(2,1)} %bitcast.6, bf16[2,160,2560]{2,1,0:T(8,128)(2,1)} %wb_ref.1, bf16[2,480,2560]{2,1,0:T(8,128)(2,1)} %bitcast.7, ...), custom_call_target="tpu_custom_call" | custom-call | tf_op jit(solution)/shard_map/att0_0/pallas_call | solution.py:379
  153.0 168.3 %mlp_0.1 = (bf16[192,2560]{1,0:T(8,128)(2,1)}, bf16[8,480,2560]{2,1,0:T(8,128)(2,1)}, bf16[8,160,2560]{2,1,0:T(8,128)(2,1)}) custom-call(bf16[192,2560]{1,0:T(8,128)(2,1)} %get-tuple-element.11.refs_0_, f32[2,2560]{1,0:T(2,128)} %refs_1_.5, bf16[2,2560,640]{2,1,0:T(8,128)(2,1)} %refs_2_.3, ...), custom_call_target="tpu_custom_call", output_to_operand_aliasing={{1}: (4, {}), {2}: (5, {})} | custom-call | tf_op jit(solution)/shard_map/mlp_0/pallas_call | solution.py:379
  321.2 32.3 %local_1.1.refs_0_ = bf16[192,2560]{1,0:T(8,128)(2,1)} custom-call(bf16[192,2560]{1,0:T(8,128)(2,1)} %get-tuple-element.14.x_ref, f32[2,2560]{1,0:T(2,128)} %g_ref.1, bf16[2,480,2560]{2,1,0:T(8,128)(2,1)} %bitcast.8, bf16[2,160,2560]{2,1,0:T(8,128)(2,1)} %wb_ref.1, bf16[8,480,2560]{2,1,0:T(8,128)(2,1)} %get-tuple-element.15.gq_ref, ...), custom_call_target="tpu_custom_call" | custom-call | tf_op jit(solution)/shard_map/local_1/pallas_call | solution.py:493
  353.5 160.2 %mlp_1.1.x_ref = bf16[192,2560]{1,0:T(8,128)(2,1)} custom-call(bf16[192,2560]{1,0:T(8,128)(2,1)} %local_1.1.refs_0_, f32[2,2560]{1,0:T(2,128)} %refs_1_.5, bf16[2,2560,640]{2,1,0:T(8,128)(2,1)} %refs_2_.3, bf16[2,640,2560]{2,1,0:T(8,128)(2,1)} %refs_3_.5), custom_call_target="tpu_custom_call" | custom-call | tf_op jit(solution)/shard_map/mlp_1/pallas_call | solution.py:379
  513.7 82.3 %gather.1 = bf16[3072,2560]{1,0:T(8,128)(2,1)} custom-call(bf16[192,2560]{1,0:T(8,128)(2,1)} %mlp_1.1.x_ref), custom_call_target="tpu_custom_call" | custom-call | tf_op jit(solution)/shard_map/gather/pallas_call | solution.py:583
  596.0 13.3 %copy.13 = bf16[48,64,2560]{2,1,0:T(8,128)(2,1)} copy(bf16[48,64,2560]{2,1,0:T(8,128)(2,1)} %bitcast.5) | data formatting | bytes 31457280

commit v3 on v0

v3 whole, which is shorter than its diff:
```python
import functools
import math

import jax
import jax.numpy as jnp
from jax import lax
from jax.experimental import pallas as pl
from jax.experimental.pallas import tpu as pltpu
from jax.sharding import PartitionSpec as P

EPS = 1e-5
MESH = pl.DeviceIdType.MESH
F32 = jnp.float32
BF16 = jnp.bfloat16
VMEM_LIMIT = 63 * 1024 * 1024


def _dot(a, b, ca, cb):
    return lax.dot_general(a, b, (((ca,), (cb,)), ((), ())), preferred_element_type=F32)


def _ln_rows(load, store, g, rows):
    def body(i, _):
        r = pl.ds(pl.multiple_of(i * 16, 16), 16)
        xf = load(r).astype(F32)
        d = xf - jnp.mean(xf, axis=-1, keepdims=True)
        var = jnp.mean(d * d, axis=-1, keepdims=True)
        store(r, (d * lax.rsqrt(var + EPS) * g).astype(BF16))
        return 0

    lax.fori_loop(0, rows // 16, body, 0)


def _place(nz):
    t = lax.axis_index("tp")
    z, c = t // 2, t % 2
    return t, z, c


def _chip(z, c, nz, sign, steps):
    fwd = sign * (1 - 2 * c) * steps
    return ((z + fwd + 8 * nz) % nz) * 2 + c


def _barrier(ids, nd=1):
    sem = pltpu.get_barrier_semaphore()
    for i in ids:
        pl.semaphore_signal(sem, inc=1, device_id={"tp": i}, device_id_type=MESH)
    if nd > 1:
        d = lax.axis_index("dp")

        def one(e, _):
            pl.semaphore_signal(sem, inc=1, device_id={"dp": (d + e) % nd, "tp": lax.axis_index("tp")}, device_id_type=MESH)
            return 0

        lax.fori_loop(1, nd, one, 0)
    pl.semaphore_wait(sem, len(ids) + nd - 1)


def _block(ref, d, nd, rows, cols):
    a = math.gcd(nd, 20)
    b = nd // a
    r, c = rows // a, cols // b
    return ref.at[pl.ds(pl.multiple_of((d // b) * r, 8), r), pl.ds(pl.multiple_of((d % b) * c, 128), c)]


class _Prefetch:
    def __init__(self, nz, nd, place, srcs, dsts, sems):
        self.nz, self.nd = nz, nd
        self.t, self.z, self.c = place
        self.d = lax.axis_index("dp")
        self.srcs, self.dsts = srcs, dsts
        self.ring_send, self.ring_recv, self.peer_send, self.peer_recv = sems

    def part(self, j, s, d):
        sign = 1 - 2 * j
        chip = _chip(self.z, self.c, self.nz, -sign, s) // 2
        ref = self.dsts[j].at[chip]
        return _block(ref, d, self.nd, ref.shape[0], ref.shape[1])

    def ring(self, j, s, first=False):
        if first:
            ref = self.srcs[j]
            src = _block(ref, self.d, self.nd, ref.shape[0], ref.shape[1])
        else:
            src = self.part(j, s, self.d)
        return pltpu.make_async_remote_copy(
            src_ref=src, dst_ref=self.part(j, s, self.d), send_sem=self.ring_send.at[j, s], recv_sem=self.ring_recv.at[j, s + 1],
            device_id={"tp": _chip(self.z, self.c, self.nz, 1 - 2 * j, 1)}, device_id_type=MESH)

    def peer(self, j, s, e):
        mine = self.part(j, s, self.d)
        return pltpu.make_async_remote_copy(
            src_ref=mine, dst_ref=mine, send_sem=self.peer_send.at[j, s, e], recv_sem=self.peer_recv.at[j, s, e],
            device_id={"dp": (self.d + e) % self.nd, "tp": self.t}, device_id_type=MESH)

    def start_ring(self):
        for j in (0, 1):
            self.ring(j, 0, True).start()

    def arrived(self, s):
        for j in (0, 1):
            self.ring(j, s - 1).wait_recv()

            @pl.when(s < self.nz - 1)
            def _():
                self.ring(j, s).start()

    def to_peers(self, s):
        def one(e, _):
            for j in (0, 1):
                self.peer(j, s, e).start()
            return 0

        lax.fori_loop(1, self.nd, one, 0)

    def drain_peers(self, lo, hi):
        def one(i, _):
            s, e = lo + i // (self.nd - 1), 1 + i % (self.nd - 1)
            for j in (0, 1):
                self.peer(j, s, e).wait()
            return 0

        lax.fori_loop(0, (hi - lo) * (self.nd - 1), one, 0)

    def drain_ring(self):
        def one(s, _):
            for j in (0, 1):
                self.ring(j, s).wait_send()
            return 0

        lax.fori_loop(0, self.nz - 1, one, 0)


def _kernel(nz, nd, names, *refs):
    R = dict(zip(names, refs, strict=True))
    x_ref, g1_ref, g2_ref, wt_ref, wo_ref, w1_ref, w2_ref, out_ref = (
        R[n] for n in ("x", "g1", "g2", "wt", "wo", "w1", "w2", "out"))
    abuf, pbuf, rbuf, wa, wb, lw, lo, la, own32, p32, mid, hid, ot, tsend, trecv = (
        R[n] for n in ("abuf", "pbuf", "rbuf", "wa", "wb", "lw", "lo", "la", "own32", "p32", "mid", "hid", "ot", "tsend", "trecv"))
    t, z, c = _place(nz)
    peer = t + 1 - 2 * c
    rows, width = own32.shape
    na, nb = wt_ref.shape[1], wo_ref.shape[1]
    ff = w1_ref.shape[2]
    hd = na // 6
    seq = rows // 3
    last = nz - 1
    streams = ((0, seq, 1), (seq, seq, 1), (2 * seq, seq // 2, -1), (2 * seq + seq // 2, seq // 2, -1))
    ks = range(len(streams))
    nxt = [_chip(z, c, nz, sg, 1) for _, _, sg in streams]
    pre = _Prefetch(nz, nd, (t, z, c), [wt_ref.at[1], wo_ref.at[1]], [R["gq"], R["go"]],
                    [R[n] for n in ("pr_send", "pr_recv", "pp_send", "pp_recv")])

    def to_peer(src, dst, send, recv):
        return pltpu.make_async_remote_copy(
            src_ref=src, dst_ref=dst, send_sem=send, recv_sem=recv, device_id={"tp": peer}, device_id_type=MESH)

    def at(buf, s, r0, n):
        return buf.at[pl.ds(pl.multiple_of(s * rows + r0, 32), n)]

    def rd(s, r0, n):
        return pl.ds(pl.multiple_of(s * rows + r0, 32), n)

    def loop(lo_, hi_, f):
        lax.fori_loop(lo_, hi_, lambda i, _: (f(i), 0)[1], 0)

    def weight(i, l, across=False):
        src, lo_, hi_ = (
            (wt_ref, lw.at[pl.ds(0, na)], lw.at[pl.ds(na, na)]),
            (wo_ref, lo.at[pl.ds(0, nb)], lo.at[pl.ds(nb, nb)]),
            (w1_ref, wa.at[:, pl.ds(0, ff)], wa.at[:, pl.ds(ff, ff)]),
            (w2_ref, wb.at[pl.ds(0, ff)], wb.at[pl.ds(ff, ff)]),
        )[i]
        j = i + 2 * l
        if across:
            return to_peer(src.at[l], hi_, R["wsend"].at[j], R["wrecv"].at[j])
        return pltpu.make_async_copy(src.at[l], lo_, R["w_sem"].at[j])

    def x_copy(k, s):
        r0, nr, sg = streams[k]
        dev = _chip(z, c, nz, -sg, s)
        return pltpu.make_async_copy(at(x_ref, dev, r0, nr), at(abuf, s, r0, nr), R["x_sem"].at[k, s])

    def ag_copy(ph, k, s):
        r0, nr, _ = streams[k]
        return pltpu.make_async_remote_copy(
            src_ref=at(abuf, s, r0, nr), dst_ref=at(abuf, s + 1, r0, nr),
            send_sem=R["ag_send"].at[ph, k, s], recv_sem=R["ag_recv"].at[ph, k, s + 1],
            device_id={"tp": nxt[k]}, device_id_type=MESH)

    def rs_copy(ph, k, s):
        r0, nr, _ = streams[k]
        return pltpu.make_async_remote_copy(
            src_ref=at(pbuf, s, r0, nr), dst_ref=at(rbuf, s, r0, nr),
            send_sem=R["rs_send"].at[ph, k, s], recv_sem=R["rs_recv"].at[ph, k, s],
            device_id={"tp": nxt[k]}, device_id_type=MESH)

    def normalise(g, r0, n):
        def load(r):
            return own32[pl.ds(pl.multiple_of(r0 + r.start, 16), 16), :]

        def store(r, v):
            abuf[pl.ds(pl.multiple_of(r0 + r.start, 16), 16), :] = v

        _ln_rows(load, store, g, n)

    def reduce_step(ph, s):
        for k in ks:
            r0, nr, _ = streams[k]

            @pl.when(s == 1)
            def _():
                pbuf[rd(s, r0, nr), :] = p32[pl.ds(r0, nr), :].astype(BF16)

            @pl.when(s > 1)
            def _():
                rs_copy(ph, k, s - 1).wait_recv()
                pbuf[rd(s, r0, nr), :] = (p32[pl.ds(r0, nr), :] + rbuf[rd(s - 1, r0, nr), :].astype(F32)).astype(BF16)

            rs_copy(ph, k, s).start()

    def finish(ph, k):
        r0, nr, _ = streams[k]
        rs_copy(ph, k, last).wait_recv()
        v = (own32[pl.ds(r0, nr), :] + rbuf[rd(last, r0, nr), :].astype(F32)).astype(BF16)
        own32[pl.ds(r0, nr), :] = v.astype(F32)
        return v

    def mlp(s):
        t1, t2 = 256, 512

        def hidden(n):
            cc = pl.ds(pl.multiple_of(n * t1, t1), t1)
            hid[:, cc] = jax.nn.gelu(_dot(abuf[rd(s, 0, rows), :], wa[:, cc], 1, 0), approximate=True).astype(BF16)

        loop(0, 2 * ff // t1, hidden)

        def cols(n):
            cc = pl.ds(pl.multiple_of(n * t2, t2), t2)
            p32[:, cc] = _dot(hid[...], wb[:, cc], 1, 0)

        loop(0, width // t2, cols)

    def mask(n):
        key = lax.broadcasted_iota(jnp.int32, (n, n), 0)
        query = lax.broadcasted_iota(jnp.int32, (n, n), 1)
        return (key <= query) & (key // seq == query // seq)

    def head(base, cc, visible):
        q = mid[pl.ds(pl.multiple_of(base, 16), hd), cc]
        k = mid[pl.ds(pl.multiple_of(base + hd, 16), hd), cc]
        v = mid[pl.ds(pl.multiple_of(base + 2 * hd, 16), hd), cc]
        sc = jnp.where(visible, _dot(k, q, 0, 0) * (hd ** -0.5), -jnp.inf)
        e = jnp.exp(sc - jnp.max(sc, axis=0, keepdims=True))
        p = (e / jnp.sum(e, axis=0, keepdims=True)).astype(BF16)
        return _dot(v, p, 1, 0).astype(BF16)

    def attend_all(s, visible):
        mid[:, pl.ds(0, rows)] = _dot(lw[pl.ds(0, 2 * na), :], abuf[rd(s, 0, rows), :], 1, 1).astype(BF16)

        def one(h):
            ot[pl.ds(pl.multiple_of(h * hd, 16), hd), pl.ds(0, rows)] = head(h * (3 * hd), pl.ds(0, rows), visible)

        loop(0, 4, one)
        tile = 512

        def cols(n):
            cc = pl.ds(pl.multiple_of(n * tile, tile), tile)
            p32[:, cc] = _dot(ot[pl.ds(0, 2 * nb), pl.ds(0, rows)], lo[pl.ds(0, 2 * nb), cc], 0, 0)

        loop(0, width // tile, cols)

    _barrier([_chip(z, c, nz, 1, 1), _chip(z, c, nz, -1, 1), peer], nd)

    for i in range(nz):
        for k in ks:
            x_copy(k, (i + 1) % nz).start()
    pre.start_ring()
    for i in range(4):
        weight(i, 0).start()
        weight(i, 0, True).start()
    for i in (0, 1):
        weight(i, 0).wait()
        weight(i, 0, True).wait_recv()
    visible = mask(rows)
    g = g1_ref[pl.ds(0, 1), :]

    def att_step(i):
        s = i + ((9 - i) // 8) * (1 - 2 * i)

        @pl.when(i > 0)
        def _():
            pre.arrived(i)
            pre.to_peers(i)

        for k in ks:
            x_copy(k, s).wait()

        @pl.when(s == 0)
        def _():
            own32[...] = abuf[pl.ds(0, rows), :].astype(F32)

        def load(r):
            return abuf[pl.ds(pl.multiple_of(s * rows + r.start, 16), 16), :]

        def store(r, v):
            abuf[pl.ds(pl.multiple_of(s * rows + r.start, 16), 16), :] = v

        _ln_rows(load, store, g, rows)
        attend_all(s, visible)

        @pl.when(s == 0)
        def _():
            own32[...] += p32[...]

        @pl.when(s > 0)
        def _():
            reduce_step(0, s)

    loop(0, nz, att_step)

    def mlp_phase(l):
        for i in (2, 3):
            weight(i, l).wait()
            weight(i, l, True).wait_recv()

        def step(s):
            @pl.when(s > 0)
            def _():
                for k in ks:
                    ag_copy(l, k, s - 1).wait_recv()

                    @pl.when(s < last)
                    def _():
                        ag_copy(l, k, s).start()

            mlp(s)

            @pl.when(s == 0)
            def _():
                own32[...] += p32[...]

            @pl.when(s > 0)
            def _():
                reduce_step(1 + l, s)

        loop(0, nz, step)

    def drain_rs(ph):
        loop(1, nz, lambda s: [rs_copy(ph, k, s).wait_send() for k in ks])

    def drain_ag(ph):
        loop(0, last, lambda s: [ag_copy(ph, k, s).wait_send() for k in ks])

    def release(ph):
        drain_ag(ph)
        for sg in (1, -1):
            pl.semaphore_signal(R["free"].at[ph], inc=1, device_id={"tp": _chip(z, c, nz, sg, 1)}, device_id_type=MESH)

    g = g2_ref[pl.ds(0, 1), :]
    for k in ks:
        finish(0, k)
        normalise(g, streams[k][0], streams[k][1])
        ag_copy(0, k, 0).start()
    drain_rs(0)
    mlp_phase(0)

    def shard(j, chip, here=False):
        dst, ref, own, sem, n, slots = ((lw, R["gq"], wt_ref, R["lw_sem"], na, 4), (lo, R["go"], wo_ref, R["lo_sem"], nb, nz))[j]
        d = dst.at[pl.ds(pl.multiple_of((chip % slots) * n, 16), n)]
        return pltpu.make_async_copy(own.at[1] if here else ref.at[chip], d, sem.at[chip])

    def start_shard(j, chip):
        @pl.when(chip == z)
        def _():
            shard(j, chip, True).start()

        @pl.when(chip != z)
        def _():
            shard(j, chip).start()

    pre.drain_ring()
    pre.drain_peers(1, nz)
    loop(0, 4, lambda chip: start_shard(0, chip))
    loop(0, nz, lambda chip: start_shard(1, chip))
    g = g1_ref[pl.ds(1, 1), :]
    for i in range(4):
        weight(i, 0, True).wait_send()
    ready = R["ready"]
    pl.semaphore_signal(ready, inc=1, device_id={"tp": peer}, device_id_type=MESH)
    for k in ks:
        finish(1, k)
        r0, nr, _ = streams[k]

        def load(r, r0=r0):
            return own32[pl.ds(pl.multiple_of(r0 + r.start, 16), 16), :]

        def store(r, v, r0=r0):
            la[pl.ds(pl.multiple_of(r0 + r.start, 16), 16), :] = v

        _ln_rows(load, store, g, nr)
    pl.semaphore_wait(ready, 1)
    swap = to_peer(la.at[pl.ds(0, rows)], la.at[pl.ds(rows, rows)], R["a_send"], R["a_recv"])
    swap.start()
    for i in (2, 3):
        weight(i, 1).start()
        weight(i, 1, True).start()
    drain_rs(1)
    release(0)
    swap.wait_recv()
    blk = 2 * seq
    visible = mask(blk)

    def pair(i):
        for k in (0, 1):
            shard(0, 2 * i + k).wait()
        w = lw[pl.ds(pl.multiple_of((i % 2) * 2 * na, 16), 2 * na), :]
        mid[...] = _dot(w, la[...], 1, 1).astype(BF16)

        @pl.when(i < nz // 2 - 2)
        def _():
            for k in (0, 1):
                start_shard(0, 2 * i + 4 + k)

        def one(h):
            for b in range(2 * rows // blk):
                cc = pl.ds(b * blk, blk)
                ot[pl.ds(pl.multiple_of(i * 2 * nb + h * hd, 16), hd), cc] = head(h * (3 * hd), cc, visible)

        loop(0, 4, one)

    loop(0, nz // 2, pair)
    loop(0, nz, lambda chip: shard(1, chip).wait())
    tiles = tsend.shape[0]
    tile = width // tiles

    def part(n):
        return to_peer(tsend.at[n], trecv.at[n], R["p_send"].at[n], R["p_recv"].at[n])

    def cols(n):
        cc = pl.ds(pl.multiple_of(n * tile, tile), tile)
        p = _dot(ot[...], lo[:, cc], 0, 0)
        tsend[n] = p[rows:].astype(BF16)
        part(n).start()
        own32[:, cc] += p[:rows]

    loop(0, tiles, cols)

    def add_part(n):
        cc = pl.ds(pl.multiple_of(n * tile, tile), tile)
        part(n).wait()
        own32[:, cc] = (own32[:, cc] + trecv[n].astype(F32)).astype(BF16).astype(F32)

    loop(0, tiles, add_part)
    swap.wait_send()

    g = g2_ref[pl.ds(1, 1), :]
    pl.semaphore_wait(R["free"].at[0], 2)
    for k in ks:
        normalise(g, streams[k][0], streams[k][1])
        ag_copy(1, k, 0).start()
    mlp_phase(1)

    def spot(k, s):
        r0, nr, sg = streams[k]
        return at(out_ref, _chip(z, c, nz, -sg, s), r0, nr)

    def local(k, s):
        r0, nr, _ = streams[k]
        return pltpu.make_async_copy(at(abuf, s, r0, nr), spot(k, s), R["o_sem"].at[k, s])

    def across(k, s):
        r0, nr, _ = streams[k]
        return to_peer(at(abuf, s, r0, nr), spot(k, s), R["o_send"].at[k, s], R["o_recv"].at[k, s])

    release(1)
    for k in ks:
        r0, nr, _ = streams[k]
        abuf[pl.ds(r0, nr), :] = finish(2, k)
        if k == 0:
            pl.semaphore_wait(R["free"].at[1], 2)
        ag_copy(2, k, 0).start()
    for k in ks:
        local(k, 0).start()
        across(k, 0).start()
    drain_rs(2)
    for i in (2, 3):
        weight(i, 1, True).wait_send()

    def out_step(s):
        for k in ks:
            ag_copy(2, k, s - 1).wait_recv()

            @pl.when(s < last)
            def _():
                ag_copy(2, k, s).start()

            local(k, s).start()
            across(k, s).start()

    loop(1, nz, out_step)
    drain_ag(2)

    def drain_out(s):
        for k in ks:
            local(k, s).wait()
            across(k, s).wait()

    loop(0, nz, drain_out)


def _call(nz, nd, x, g1, g2, wt, wo, w1, w2):
    tokens, width = x.shape
    rows = tokens // (2 * nz)
    na, nb, ff = wt.shape[1], wo.shape[1], w1.shape[2]
    nk, tiles = 4, 5
    vmem, hbm = pl.BlockSpec(memory_space=pltpu.VMEM), pl.BlockSpec(memory_space=pl.ANY)
    dma = pltpu.SemaphoreType.DMA
    ins = [("x", x, hbm), ("g1", g1, vmem), ("g2", g2, vmem), ("wt", wt, hbm), ("wo", wo, hbm), ("w1", w1, hbm), ("w2", w2, hbm)]
    outs = [("out", x.shape), ("gq", (nz, na, width)), ("go", (nz, nb, width))]
    vm = [("abuf", (nz * rows, width)), ("pbuf", (nz * rows, width)), ("rbuf", (nz * rows, width)),
          ("wa", (width, 2 * ff)), ("wb", (2 * ff, width)), ("lw", (4 * na, width)), ("lo", (nz * nb, width)),
          ("la", (2 * rows, width)), ("mid", (2 * na, 2 * rows)), ("hid", (rows, 2 * ff)), ("ot", (nz * nb, 2 * rows)),
          ("tsend", (tiles, rows, width // tiles)), ("trecv", (tiles, rows, width // tiles))]
    sems = [("x_sem", (nk, nz)), ("w_sem", (6,)), ("wsend", (6,)), ("wrecv", (6,)),
            ("ag_send", (3, nk, nz)), ("ag_recv", (3, nk, nz)), ("rs_send", (3, nk, nz)), ("rs_recv", (3, nk, nz)),
            ("pr_send", (2, nz)), ("pr_recv", (2, nz)), ("pp_send", (2, nz, nd)), ("pp_recv", (2, nz, nd)),
            ("lw_sem", (nz,)), ("lo_sem", (nz,)), ("a_send", ()), ("a_recv", ()), ("p_send", (tiles,)), ("p_recv", (tiles,)),
            ("o_sem", (nk, nz)), ("o_send", (nk, nz)), ("o_recv", (nk, nz))]
    scratch = [(n, pltpu.VMEM(sh, BF16)) for n, sh in vm]
    scratch += [("own32", pltpu.VMEM((rows, width), F32)), ("p32", pltpu.VMEM((rows, width), F32))]
    scratch += [(n, dma(sh) if sh else dma) for n, sh in sems] + [("ready", pltpu.SemaphoreType.REGULAR), ("free", pltpu.SemaphoreType.REGULAR((2,)))]
    names = [e[0] for e in ins + outs + scratch]
    return pl.pallas_call(
        functools.partial(_kernel, nz, nd, names),
        out_shape=[jax.ShapeDtypeStruct(sh, BF16) for _, sh in outs],
        in_specs=[e[2] for e in ins],
        out_specs=[hbm] * len(outs),
        scratch_shapes=[e[1] for e in scratch],
        compiler_params=pltpu.CompilerParams(collective_id=0, has_side_effects=True, vmem_limit_bytes=VMEM_LIMIT),
        name="layers",
    )(*[e[1] for e in ins])[0]


def solution(mesh):
    n = mesh.shape["tp"]

    def body(x, g1, g2, wqkv, wo, w1, w2):
        b, s, d = x.shape
        layers, _, hl, hd3 = wqkv.shape
        wt = wqkv.transpose(0, 2, 3, 1).reshape(layers, hl * hd3, d)
        return _call(n // 2, mesh.shape["dp"], x.reshape(b * s, d), g1, g2, wt, wo, w1, w2).reshape(b, s, d)

    in_specs = (P("dp"), P(), P(), P(None, None, "tp", None), P(None, "tp", None), P(None, None, "tp"), P(None, "tp", None))
    return jax.shard_map(body, mesh=mesh, in_specs=in_specs, out_specs=P("dp"), check_vma=False)
```

time: 1030 us -> 578 us (0.56)
  waiting for transfers between devices: 730 us -> 0 us
  Pallas kernels: 0 us -> 564 us
  matrix products: 125 us -> 0 us
  other arithmetic: 97.7 us -> 0 us
  local copies, waits for them, and re-layouts: 58.1 us -> 13.3 us
  between operations: 13.8 us -> 0.01 us
    psum x4 -> x0, waiting for transfers between devices: 730 us -> none  [the longest x2 367 us: body(): lax.psum(pa, 'tp').astype(jnp.float32)]
    pallas_call x0 -> x1, Pallas kernels: none -> 564 us  [_call(): pl.pallas_call(functools.partial(_kernel, nz, nd, names), out_shape=[jax....]
    dot_general x10 -> x0, matrix products: 125 us -> none  [the longest x2 79.7 us: body(): jnp.dot(m, w2[l], preferred_element_type=jnp.float32).astype(jnp.bfloat16)]
    reduce_sum x8 -> x0, other arithmetic: 71.2 us -> none  [the longest x4 48.2 us: _ln(): mu = jnp.mean(xf, axis=-1, keepdims=True)]
    convert_element_type x2 -> x0, other arithmetic: 22.9 us -> none  [the longest x1 17.3 us: body(): (h.astype(jnp.float32) + lax.psum(pm, 'tp').astype(jnp.float32)).astype(j...]
    reshape x4 -> x0, local copies, waits for them, and re-layouts: 16.8 us -> none  [the longest x2 13.5 us: body(): qkv = qkv.astype(jnp.bfloat16).reshape(b, s, hl, 3, hd)]
    slice x5 -> x0, local copies, waits for them, and re-layouts: 14.5 us -> none  [the longest x2 11.3 us: _attention(): qkv[:, :, :, 2]]
    unnamed x32 -> x1, local copies, waits for them, and re-layouts: 23.3 us -> 13.3 us
  transfers between devices with their start and end apart: 4 -> 0, of which waited for: 4 -> 0; matrix products, arithmetic and copies ran while one was open for 0% -> 0% of each run, Pallas kernels for 0% -> 0%
where the time goes in v3:
time: 578 us; the launch traced here: 577 us
  Pallas kernels  564 us (98%)
  local copies, waits for them, and re-layouts  13.3 us (2%)
    pallas_call x1, Pallas kernels, _call(): pl.pallas_call(functools.partial(_kernel, nz, nd, names), out_shape=[jax....  564 us
    unnamed x1, local copies, waits for them, and re-layouts  13.3 us

profile of v3, /device:TPU:21, one launch (start us, length us, event | category | flops | bytes accessed | tf_op | source)
XLA Modules:
  0.0 577.4 jit_solution(11096596333975514464)
XLA Ops:
  0.0 564.1 %layers.1 = (bf16[3072,2560]{1,0:T(8,128)(2,1)}, bf16[8,480,2560]{2,1,0:T(8,128)(2,1)}, bf16[8,160,2560]{2,1,0:T(8,128)(2,1)}) custom-call(bf16[3072,2560]{1,0:T(8,128)(2,1)} %bitcast.5, f32[2,2560]{1,0:T(2,128)} %refs_1_.1, f32[2,2560]{1,0:T(2,128)} %refs_2_.1, bf16[2,480,2560]{2,1,0:T(8,128)(2,1)} %bitcast.7, bf16[2,160,2560]{2,1,0:T(8,128)(2,1)} %refs_4_.1, ...), custom_call_target="tpu_custom_call" | custom-call | tf_op jit(solution)/shard_map/layers/pallas_call | solution.py:535
  564.1 13.3 %copy.9 = bf16[48,64,2560]{2,1,0:T(8,128)(2,1)} copy(bf16[48,64,2560]{2,1,0:T(8,128)(2,1)} %bitcast.6) | data formatting | bytes 31457280
